TPU v7x, 256 devices: a whole 4x4x8 slice. The times are simulated.
256 devices in a mesh: dp: 4 (over y), expert: 64 (over z, x, core).
Axes of the slice: x: 4, y: 4, z: 8, core: 2. Of those that a mesh axis runs over, the one named last changes fastest.
Arguments:
- grad_out: bfloat16 [32768, 3072], P(('dp', 'expert')), may hold values from -6 to 6
- expert_ids: int32 [32768, 2], P(('dp', 'expert')), may hold values from 0 to 7, all different within a row; in each aligned block of 128 rows (0 to 127, 128 to 255, ...) at most 36 rows name the same one
- down_weight: bfloat16 [64, 1024, 3072], P('expert'), may hold values from -0.109375 to 0.109375
- history_grad: float32 [8, 8], replicated, may hold values from 0.5 to 3
- history_hidden: float32 [8, 8], replicated, may hold values from 0.5 to 3
Outputs:
- hidden_scaled: bfloat16 [4, 64, 2304, 1024], P('dp', 'expert')
- new_history_grad: float32 [8, 8], replicated
- new_history_hidden: float32 [8, 8], replicated
Inputs may be any that keep to these rules, and one draw needn't show every extreme that they name: `expert_ids`: each row names 2 different experts; among the 128 rows of one device no expert is named more than 36 times, a bound that some block reaches in some devices.
All inputs are finite; a program needn't handle non-finite values.
Results may differ from a plain program's by a relative error of at most 0.0045.
Values may be sent and summed in bfloat16 or wider, within the bound.
A program may use at most 128 MiB of HBM per device.

v0:
```python
import functools

import jax
import jax.numpy as jnp
from jax import lax
from jax.sharding import Mesh
from jax.sharding import PartitionSpec as P

EXPERT = ("expert_0", "expert_1", "expert_2")
DP_EXPERT = ("dp", "expert_0", "expert_1", "expert_2")


def from_partner(shard, axis, apart):
    return lax.ppermute(shard, axis, [(i, i ^ 1 << apart) for i in range(lax.axis_size(axis))])


def by_axis(shard, axes):
    return functools.reduce(lax.pmax, axes, shard)


def per_device(grad_out, expert_ids, down_weight, history_grad, history_hidden):
    tok_rows = grad_out.shape[0]
    features = grad_out.shape[1]
    experts = history_grad.shape[1]
    slices = lax.axis_size(EXPERT) // experts
    capacity = tok_rows * 9 // 32
    flat_ids = expert_ids.reshape(-1)
    onehot = (flat_ids[:, None] == jnp.arange(experts, dtype=jnp.int32)[None, :]).astype(jnp.int32)
    before = jnp.cumsum(onehot, axis=0) - onehot
    slot_index = jnp.sum(before * onehot, axis=1)
    target = flat_ids * capacity + slot_index
    matches = (jnp.arange(experts * capacity, dtype=jnp.int32)[:, None] == target[None, :]).astype(
        jnp.int32
    )
    dispatch = jnp.sum(matches.reshape(experts * capacity, tok_rows, 2), axis=2).astype(
        jnp.bfloat16
    )
    gathered = jnp.dot(dispatch, grad_out, preferred_element_type=jnp.float32)
    scale_in = 1.0 / jnp.max(history_grad, axis=0)
    scale_hidden = 1.0 / jnp.max(history_hidden, axis=0)
    quantized = jnp.clip(
        gathered.reshape(experts, capacity, -1) * scale_in[:, None, None], -1.0, 1.0
    ).astype(jnp.bfloat16)
    own_index = lax.axis_index(EXPERT)
    own_expert = own_index // slices
    chosen = jnp.arange(experts, dtype=jnp.int32) == own_expert
    own_scale_in = jnp.sum(jnp.where(chosen, scale_in, 0.0))
    own_scale_hidden = jnp.sum(jnp.where(chosen, scale_hidden, 0.0))
    routed = jnp.max(onehot.reshape(tok_rows, 2, experts), axis=1) > 0
    row_peak = jnp.max(jnp.abs(grad_out.astype(jnp.float32)), axis=1)
    grad_peak = jnp.max(jnp.where(routed, row_peak[:, None], 0.0), axis=0)
    weight_block = down_weight[0]
    width = features // slices
    pieces = quantized.reshape(experts, capacity, slices, width).transpose(0, 2, 1, 3)
    pieces = pieces.reshape(experts * slices, capacity, width)
    arrived = lax.all_to_all(pieces, EXPERT, split_axis=0, concat_axis=0, tiled=True)
    collected = arrived[None]
    member = own_index % slices
    for bit in range(slices.bit_length() - 1):
        partner = from_partner(collected, EXPERT, bit)
        upper = member // (1 << bit) % 2 == 1
        first = jnp.where(upper, partner, collected)
        second = jnp.where(upper, collected, partner)
        collected = jnp.concatenate([first, second], axis=0)
    weight_parts = weight_block.reshape(weight_block.shape[0], slices, width)
    product = jnp.einsum(
        "jsic,ujc->siu", collected, weight_parts, preferred_element_type=jnp.float32
    )
    hidden = product / own_scale_in
    hidden_peak = jnp.max(jnp.abs(hidden))
    hidden_vec = jnp.where(chosen, hidden_peak, 0.0)
    grad_amax, hidden_amax = (by_axis(grad_peak, DP_EXPERT), by_axis(hidden_vec, DP_EXPERT))
    scaled = jnp.clip(hidden * own_scale_hidden, -1.0, 1.0).astype(jnp.bfloat16)
    hidden_scaled = scaled.reshape(1, 1, -1, scaled.shape[2])
    new_history_grad = jnp.concatenate([history_grad[1:], grad_amax[None, :]], axis=0)
    new_history_hidden = jnp.concatenate([history_hidden[1:], hidden_amax[None, :]], axis=0)
    return (hidden_scaled, new_history_grad, new_history_hidden)


def solution(mesh):
    split = Mesh(
        mesh.devices.reshape(mesh.shape["dp"], 8, 4, 2), ("dp", "expert_0", "expert_1", "expert_2")
    )
    placed = (P(DP_EXPERT, None), P(DP_EXPERT, None), P(EXPERT, None, None), P(), P())
    return jax.shard_map(
        per_device,
        mesh=split,
        in_specs=placed,
        out_specs=(P("dp", EXPERT, None, None), P(), P()),
        check_vma=False,
    )
```

profile of v0, /device:TPU:1, one launch (start us, length us, event | category | flops | bytes accessed | tf_op | source)
XLA Modules:
  0.0 402.4 jit_solution(8138557656328672545)
XLA Ops:
  0.6 0.8 copy.38
  1.7 0.6 reduce-window.6
  2.9 0.7 multiply_add_fusion
  3.6 1.7 fusion.11
  5.4 0.7 copy.46
  6.1 0.6 select_reduce_fusion.1
  6.7 0.4 fusion.10
  7.5 59.8 %all_to_all.5 = bf16[64,36,384]{2,1,0:T(8,128)(2,1)S(1)} all-to-all(bf16[64,36,384]{2,1,0:T(8,128)(2,1)S(1)} %bitcast.37), channel_id=1, replica_groups=mesh['dp'=4,'expert_0'=8,'expert_1'=4,'expert_2'=2] {'expert_0','expert_..., dimensions={0} | all-to-all | bytes 3538944 | tf_op jit(solution)/shard_map/all_to_all | solution.py:56
  67.3 1.5 copy.59
  68.8 1.9 collective-permute-start
  70.7 3.7 collective-permute-done
  74.4 2.0 broadcast_select_fusion.5
  76.8 0.8 copy-done.1
  77.6 0.6 copy-done.2
  78.2 1.2 collective-permute-start.1
  79.4 76.6 %collective-permute-done.1 = bf16[2,64,36,384]{3,1,0,2:T(8,128)(2,1)} collective-permute-done((bf16[2,64,36,384]{3,1,0,2:T(8,128)(2,1)S(1)}, bf16[2,64,36,384]{3,1,0,2:T(8,128)(2,1)}, u32[]{:S(2)}, u32[]{:S(2)}) %collective-permute-start.1) | collective-permute-done | bytes 3538976 | tf_op jit(solution)/shard_map/ppermute | solution.py:14
  156.0 4.6 %broadcast_select_fusion.3 = (bf16[2,64,36,384]{3,1,0,2:T(8,128)(2,1)S(1)}, bf16[2,64,36,384]{3,1,0,2:T(8,128)(2,1)}) fusion(bf16[2,64,36,384]{3,1,0,2:T(8,128)(2,1)} %collective-permute-done.1, pred[]{:T(512)S(6)} %eq.67, bf16[1,64,36,384]{3,1,0,2:T(8,128)(2,1)} %copy-done.2, bf16[1,64,36,384]{3,1,0,2:T(8,128)(2,1)} %copy-done.1), kind=kLoop, calls=%fused_computation.15 | loop fusion | flops 5308416 | bytes 14155777 | tf_op jit(solution)/shard_map/jit(_where)/select_n | solution.py:62
  160.6 5.8 %pad_maximum_fusion = bf16[4,64,36,384]{3,1,0,2:T(8,128)(2,1)} fusion(bf16[2,64,36,384]{3,1,0,2:T(8,128)(2,1)} %get-tuple-element.18, bf16[2,64,36,384]{3,1,0,2:T(8,128)(2,1)S(1)} %get-tuple-element.17), kind=kLoop, calls=%fused_computation.7 | loop fusion | flops 3538944 | bytes 14155776 | tf_op jit(solution)/shard_map/concatenate | solution.py:64
  166.4 2.7 collective-permute-start.2
  169.2 7.2 %copy.47 = bf16[128,8,8,384]{3,2,1,0:T(8,128)(2,1)} copy(bf16[128,8,8,384]{3,1,2,0:T(8,128)(2,1)} %bitcast.38) | data formatting | bytes 12582912
  176.7 0.6 fusion.17
  177.3 143.6 %collective-permute-done.2 = bf16[4,64,36,384]{3,1,0,2:T(8,128)(2,1)} collective-permute-done((bf16[4,64,36,384]{3,1,0,2:T(8,128)(2,1)}, bf16[4,64,36,384]{3,1,0,2:T(8,128)(2,1)}, u32[]{:S(2)}, u32[]{:S(2)}) %collective-permute-start.2) | collective-permute-done | bytes 7077920 | tf_op jit(solution)/shard_map/ppermute | solution.py:14
  320.9 7.0 %broadcast_select_fusion.1 = (bf16[4,64,36,384]{3,1,0,2:T(8,128)(2,1)S(1)}, bf16[4,64,36,384]{3,1,0,2:T(8,128)(2,1)}) fusion(bf16[4,64,36,384]{3,1,0,2:T(8,128)(2,1)} %collective-permute-done.2, pred[]{:T(512)S(6)} %eq.66, bf16[2,64,36,384]{3,1,0,2:T(8,128)(2,1)S(1)} %copy-done, bf16[2,64,36,384]{3,1,0,2:T(8,128)(2,1)S(1)} %get-tuple-element.17), kind=kLoop, calls=%fused_computation.9 | loop fusion | flops 10616832 | bytes 28311552 | tf_op jit(solution)/shard_map/jit(_where)/select_n | solution.py:62
  328.0 20.9 %abs_reduce_fusion = (f32[]{:T(128)}, bf16[64,36,1024]{2,0,1:T(8,128)(2,1)S(1)}) fusion(f32[]{:T(128)} %fusion.17, f32[]{:T(128)} %get-tuple-element.11, bf16[1024,8,384]{2,1,0:T(8,128)(2,1)} %bitcast.39, bf16[4,64,36,384]{3,1,0,2:T(8,128)(2,1)} %get-tuple-element.14, bf16[4,64,36,384]{3,1,0,2:T(8,128)(2,1)S(1)} %get-tuple-element.13), kind=kOutput, calls=%fused_computation.5 | convolution fusion | flops 14516748288 | bytes 25165836 | tf_op jit(solution)/shard_map/jsic,ujc->siu/dot_general | solution.py:66
  348.9 0.6 fusion.16
  349.5 5.0 %copy.44 = bf16[64,36,1024]{2,1,0:T(8,128)(2,1)} copy(bf16[64,36,1024]{2,0,1:T(8,128)(2,1)S(1)} %get-tuple-element.16) | data formatting | bytes 9437184 | tf_op jit(solution)/shard_map/convert_element_type | solution.py:73
  354.5 7.2 %reshape.68 = bf16[1,1,2304,1024]{3,2,1,0:T(8,128)(2,1)} reshape(bf16[64,36,1024]{2,1,0:T(8,128)(2,1)} %copy.44) | data formatting | bytes 9437184 | tf_op jit(solution)/shard_map/reshape | solution.py:74
  361.7 8.7 %all-reduce.2 = (f32[8]{0:T(128)S(1)}, f32[8]{0:T(128)S(1)}) all-reduce(f32[8]{0:T(128)S(1)} %select_reduce_fusion, f32[8]{0:T(128)S(1)} %fusion.16), channel_id=1, replica_groups=mesh['dp'=4,'expert_0'=8,'expert_1'=4,'expert_2'=2] {'dp'}, use_global_device_ids=true, to_apply=%region_11.12 | all-reduce | flops 16 | bytes 128 | tf_op jit(solution)/shard_map/pmax | solution.py:18
  370.4 11.6 %all-reduce = (f32[8]{0:T(128)S(1)}, f32[8]{0:T(128)S(1)}) all-reduce(f32[8]{0:T(128)S(1)} %get-tuple-element.7, f32[8]{0:T(128)S(1)} %get-tuple-element.8), channel_id=1, replica_groups=mesh['dp'=4,'expert_0'=8,'expert_1'=4,'expert_2'=2] {'expert_0'}, use_global_device_ids=true, to_apply=%region_12.13 | all-reduce | flops 16 | bytes 128 | tf_op jit(solution)/shard_map/pmax | solution.py:18
  382.0 8.0 %all-reduce.1 = (f32[8]{0:T(128)S(1)}, f32[8]{0:T(128)S(1)}) all-reduce(f32[8]{0:T(128)S(1)} %get-tuple-element.3, f32[8]{0:T(128)S(1)} %get-tuple-element.4), channel_id=1, replica_groups=mesh['dp'=4,'expert_0'=8,'expert_1'=4,'expert_2'=2] {'expert_1'}, use_global_device_ids=true, to_apply=%region_13.14 | all-reduce | flops 16 | bytes 128 | tf_op jit(solution)/shard_map/pmax | solution.py:18
  390.0 11.7 %all-reduce.3 = (f32[1,8]{1,0:T(1,128)S(1)}, f32[1,8]{1,0:T(1,128)S(1)}) all-reduce(f32[1,8]{1,0:T(1,128)S(1)} %bitcast.40, f32[1,8]{1,0:T(1,128)S(1)} %bitcast.41), channel_id=1, replica_groups=mesh['dp'=4,'expert_0'=8,'expert_1'=4,'expert_2'=2] {'expert_2'}, use_global_device_ids=true, to_apply=%region_14.15 | all-reduce | flops 16 | bytes 128 | tf_op jit(solution)/shard_map/pmax | solution.py:18
  401.8 0.6 pad_maximum_fusion.2
  (31 shorter events, 2.0 us)
Async XLA Ops:
  5.4 0.7 copy-start.4
  68.8 5.6 %collective-permute-start = (bf16[1,64,36,384]{3,1,0,2:T(8,128)(2,1)}, bf16[1,64,36,384]{3,1,0,2:T(8,128)(2,1)}, u32[]{:S(2)}, u32[]{:S(2)}) collective-permute-start(bf16[1,64,36,384]{3,1,0,2:T(8,128)(2,1)} %bitcast.34), channel_id=1, source_target_pairs={{0,1},{1,0},{2,3},{3,2},{4,5},{5,4},{6,7},{7,6},{8,9},{9,8},{10,11... | collective-permute-start | bytes 5308424 | tf_op jit(solution)/shard_map/ppermute | solution.py:14
  76.4 1.3 copy-start.1
  76.4 1.8 copy-start.2
  78.2 77.8 %collective-permute-start.1 = (bf16[2,64,36,384]{3,1,0,2:T(8,128)(2,1)S(1)}, bf16[2,64,36,384]{3,1,0,2:T(8,128)(2,1)}, u32[]{:S(2)}, u32[]{:S(2)}) collective-permute-start(bf16[2,64,36,384]{3,1,0,2:T(8,128)(2,1)S(1)} %pad_maximum_fusion.1), channel_id=1, source_target_pairs={{0,2},{1,3},{2,0},{3,1},{4,6},{5,7},{6,4},{7,5},{8,10},{9,11},{10,... | collective-permute-start | bytes 10616840 | tf_op jit(solution)/shard_map/ppermute | solution.py:14
  160.6 8.5 %copy-start.5 = (f32[8,8]{1,0:T(8,128)S(1)}, f32[8,8]{1,0:T(8,128)}, u32[]{:S(2)}) copy-start(f32[8,8]{1,0:T(8,128)} %param.9) | copy-start | bytes 772
  166.4 154.5 %collective-permute-start.2 = (bf16[4,64,36,384]{3,1,0,2:T(8,128)(2,1)}, bf16[4,64,36,384]{3,1,0,2:T(8,128)(2,1)}, u32[]{:S(2)}, u32[]{:S(2)}) collective-permute-start(bf16[4,64,36,384]{3,1,0,2:T(8,128)(2,1)} %pad_maximum_fusion), channel_id=1, source_target_pairs={{0,4},{1,5},{2,6},{3,7},{4,0},{5,1},{6,2},{7,3},{8,12},{9,13},{10,... | collective-permute-start | bytes 21233672 | tf_op jit(solution)/shard_map/ppermute | solution.py:14
  169.2 7.2 %copy-start.6 = (s32[128,2]{0,1:T(2,128)S(1)}, s32[128,2]{0,1:T(2,128)}, u32[]{:S(2)}) copy-start(s32[128,2]{0,1:T(2,128)} %param.6) | copy-start | bytes 3076
  169.2 7.2 %copy-start.3 = (bf16[128,3072]{1,0:T(8,128)(2,1)S(1)}, bf16[128,3072]{1,0:T(8,128)(2,1)}, u32[]{:S(2)}) copy-start(bf16[128,3072]{1,0:T(8,128)(2,1)} %param.5) | copy-start | bytes 2359300
  169.2 151.7 %copy-start = (bf16[2,64,36,384]{3,1,0,2:T(8,128)(2,1)S(1)}, bf16[2,64,36,384]{3,1,0,2:T(8,128)(2,1)}, u32[]{:S(2)}) copy-start(bf16[2,64,36,384]{3,1,0,2:T(8,128)(2,1)} %get-tuple-element.18) | copy-start | bytes 10616836
where the time goes:
time: 403 us; the launch traced here: 402 us
  waiting for transfers between devices  224 us (56%)
  blocking collectives  99.9 us (25%)
  local copies, waits for them, and re-layouts  24.8 us (6%)
  other arithmetic  24.5 us (6%)
  matrix products  22.7 us (6%)
  starting transfers between devices  5.83 us (1%)
    ppermute x3, waiting for transfers between devices, from_partner(): lax.ppermute(shard, axis, [(i, i ^ 1 << apart) for i in range(lax.axis_si...  224 us
    all_to_all x1, blocking collectives, per_device(): lax.all_to_all(pieces, EXPERT, split_axis=0, concat_axis=0, tiled=True)  59.8 us
    pmax x4, blocking collectives, by_axis(): return functools.reduce(lax.pmax, axes, shard)  40.1 us
    dot_general x1, matrix products, per_device(): jnp.einsum('jsic,ujc->siu', collected, weight_parts, preferred_element_ty...  20.9 us
    select_n x3, other arithmetic, per_device(): first = jnp.where(upper, partner, collected)  13.6 us
    unnamed x17, local copies, waits for them, and re-layouts  10 us
  transfers between devices with their start and end apart: 3, of which 3 were waited for; matrix products, arithmetic and copies ran while one was open for 2% of the time, Pallas kernels for 0%

commit v1 on v0

v1 whole, which is shorter than its diff:
```python
import functools

import jax
import jax.numpy as jnp
from jax import lax
from jax.experimental import pallas as pl
from jax.experimental.pallas import tpu as pltpu
from jax.sharding import PartitionSpec as P

MESH = pl.DeviceIdType.MESH
F32, BF16 = jnp.float32, jnp.bfloat16
CORES = 2
MAIN = 32
UNITS = 256


def ceil_parts(values, width, count):
    return functools.reduce(lambda a, b: a + b, [(values >= width * i).astype(jnp.int32) for i in range(1, count)])


def kernel(
    n_y, n_z, n_x, capacity,
    ids_ref, hist_grad, hist_hidden, grad_hbm, weight_hbm,
    out_hbm, new_grad, new_hidden,
    grad_v, weight_v, queue, gathered, staged, slot_of, unfold, order, grad_peak, hidden_peak, message, inbox,
    local_sem, out_sem, z_send, z_recv, x_send, x_recv, f_send, f_recv, d_send, d_recv, m_send, m_recv,
):
    tok = grad_v.shape[0]
    features = grad_v.shape[1]
    tail = capacity - MAIN
    fold = MAIN // tail
    width = features // fold
    members = n_x * CORES
    rows = members * MAIN
    extra = members * tail
    n_units = weight_v.shape[0]

    y = lax.axis_index("dp")
    me = lax.axis_index("expert")
    core = me % CORES
    x = (me // CORES) % n_x
    z = me // members
    group = me % members

    def at(to_z, to_x, to_core):
        return (y, (to_z * n_x + to_x) * CORES + to_core)

    right, left, far = (x + 1) % n_x, (x + n_x - 1) % n_x, (x + 2) % n_x
    partner = at(z, x, 1 - core)

    peers = [
        [at(z, ((group + j) % members) // CORES, ((group + j) % members) % CORES) for j in range(1, members)],
        [((y + j) % n_y, me) for j in range(1, n_y)],
        [at((z + j) % n_z, x, core) for j in range(1, n_z)],
    ]
    barrier = pltpu.get_barrier_semaphore()
    for phase in peers:
        for peer in phase:
            pl.semaphore_signal(barrier, inc=1, device_id=peer, device_id_type=MESH)

    grad_in = pltpu.make_async_copy(grad_hbm, grad_v, local_sem.at[0])
    grad_in.start()
    weight_in = pltpu.make_async_copy(weight_hbm, weight_v, local_sem.at[1])
    weight_in.start()

    def iota(shape, axis):
        return lax.broadcasted_iota(jnp.int32, shape, axis)

    ids = ids_ref[...]
    named = (iota((n_z, tok), 0) == ids[0:1, :]) | (iota((n_z, tok), 0) == ids[1:2, :])
    earlier = (iota((tok, tok), 0) < iota((tok, tok), 1)).astype(F32).astype(BF16)
    before = jnp.dot(named.astype(F32).astype(BF16), earlier, preferred_element_type=F32)
    slot_of[...] = jnp.where(named, before, -1.0)

    scale_in = 1.0 / jnp.max(hist_grad[...], axis=0, keepdims=True)
    scale_hidden = 1.0 / jnp.max(hist_hidden[...], axis=0, keepdims=True)
    own = iota((1, n_z), 1) == z
    own_in = jnp.sum(jnp.where(own, scale_in, 0.0), axis=1, keepdims=True)
    own_hidden = jnp.sum(jnp.where(own, scale_hidden, 0.0), axis=1, keepdims=True)

    all_rows = n_z * MAIN
    slots = jnp.broadcast_to(slot_of[...][:, None, :], (n_z, MAIN, tok)).reshape(all_rows, tok)
    in_block = iota((all_rows, tok), 0) % MAIN
    pick_main = (slots == in_block.astype(F32)).astype(F32).astype(BF16)
    is_tail = slots == (in_block % tail + MAIN).astype(F32)
    row_scale = jnp.sum(
        jnp.where(iota((all_rows, n_z), 1) == iota((all_rows, n_z), 0) // MAIN, scale_in, 0.0), axis=1, keepdims=True
    )

    def scaled(values):
        return jnp.clip(values * row_scale, -1.0, 1.0).astype(BF16).reshape(n_z, MAIN, width)

    def folded_peak(values):
        return functools.reduce(jnp.maximum, [jnp.abs(values[:, i:i + 128]) for i in range(0, width, 128)])

    grad_in.wait()
    tails = jnp.zeros((all_rows, width), F32)
    peak = jnp.zeros((all_rows, 128), F32)
    for part in range(fold):
        piece = grad_v[:, part * width:(part + 1) * width]
        values = jnp.dot(pick_main, piece, preferred_element_type=F32)
        queue[:, :, part * width:(part + 1) * width] = scaled(values)
        peak = jnp.maximum(peak, folded_peak(values))
        pick = (is_tail & (in_block // tail == part)).astype(F32).astype(BF16)
        tails = tails + jnp.dot(pick, piece, preferred_element_type=F32)
    queue[:, :, features:] = scaled(tails)
    peak = jnp.maximum(peak, folded_peak(tails))
    peak = jnp.max(jnp.max(peak.reshape(n_z, MAIN, 128), axis=1), axis=1, keepdims=True)
    grad_peak[...] = jnp.broadcast_to(peak, (n_z, 128))
    hidden_peak[...] = jnp.zeros_like(hidden_peak)
    gathered[0, pl.ds(pl.multiple_of(group * MAIN, MAIN), MAIN), :] = queue[z]

    goes, comes = iota((rows, rows), 0), iota((rows, rows), 1)
    wanted = (goes % extra // tail) * MAIN + (goes // extra) * tail + goes % tail
    unfold[...] = (wanted == comes).astype(F32).astype(BF16)
    half = order.shape[0]
    goes, comes = iota((half, half), 0), iota((half, half), 1)
    block = ceil_parts(goes, capacity, members // 2)
    slot = goes - block * capacity
    wanted = jnp.where(slot < MAIN, block * MAIN + slot, rows // 2 + block * tail + slot - MAIN)
    order[...] = (wanted == comes).astype(F32).astype(BF16)

    pl.semaphore_wait(barrier, sum(len(phase) for phase in peers))

    def offset(k):
        return ((k + 1) // 2) * (2 * (k % 2) - 1)

    def part_of(k, member, low=0, count=MAIN):
        start = pl.multiple_of(member * MAIN + low, MAIN // 2)
        return gathered.at[k, pl.ds(start, count), :]

    def remote(source, target, send, recv, device):
        return pltpu.make_async_remote_copy(
            src_ref=source, dst_ref=target, send_sem=send, recv_sem=recv, device_id=device, device_id_type=MESH
        )

    def z_copy(k):
        to_z = (z - offset(k) + n_z) % n_z
        return remote(queue.at[to_z], part_of(k, group), z_send.at[k], z_recv.at[k], at(to_z, x, core))

    def x_copy(k, way):
        mine = part_of(k, group)
        return remote(mine, mine, x_send.at[k, way], x_recv.at[k, way], at(z, (right, left)[way], core))

    def x_arrival(k, way):
        theirs = part_of(k, (left, right)[way] * CORES + core)
        return remote(theirs, theirs, x_send.at[k, way], x_recv.at[k, way], partner)

    def f_copy(k, way):
        theirs = part_of(k, (left, right)[way] * CORES + core, way * (MAIN // 2), MAIN // 2)
        return remote(theirs, theirs, f_send.at[k, way], f_recv.at[k, way], at(z, (right, left)[way], core))

    def f_arrival(k, way):
        theirs = part_of(k, far * CORES + core, way * (MAIN // 2), MAIN // 2)
        return remote(theirs, theirs, f_send.at[k, way], f_recv.at[k, way], partner)

    def d_copy(k, piece, whose):
        if piece < 3:
            block = part_of(k, (x, left, right)[piece] * CORES + whose)
        else:
            block = part_of(k, far * CORES + whose, (piece - 3) * (MAIN // 2), MAIN // 2)
        return remote(block, block, d_send.at[k, piece], d_recv.at[k, piece], partner)

    def z_body(k, carry):
        z_copy(k).start()
        return carry

    lax.fori_loop(1, n_z, z_body, 0)
    weight_in.wait()

    factor = own_hidden / own_in

    def out_copy(k):
        from_z = (z + offset(k) + n_z) % n_z
        start = pl.multiple_of(from_z * (members * capacity), members * capacity)
        return pltpu.make_async_copy(
            staged.at[k % 2], out_hbm.at[0, 0, pl.ds(start, members * capacity), :], out_sem.at[k % 2]
        )

    def multiply(k):
        folded = gathered[k, 0:rows, features:features + width]
        plain = jnp.dot(unfold[...], folded, preferred_element_type=F32).astype(BF16)
        for part in range(fold):
            gathered[k, rows:rows + extra, part * width:(part + 1) * width] = plain[part * extra:(part + 1) * extra]

        @pl.when(k >= 2)
        def _():
            out_copy(k - 2).wait()

        def unit_body(n, carry):
            start = pl.multiple_of(n * UNITS, UNITS)
            product = lax.dot_general(
                gathered[k, :, 0:features], weight_v[pl.ds(start, UNITS), :],
                (((1,), (1,)), ((), ())), preferred_element_type=F32,
            )
            size = jnp.abs(product).reshape((rows + extra) // 8, 8, UNITS)
            hidden_peak[...] = jnp.maximum(hidden_peak[...], jnp.max(size, axis=0))
            result = jnp.clip(product * factor, -1.0, 1.0).astype(BF16)
            for side in range(2):
                low, low_extra = side * (rows // 2), rows + side * (extra // 2)
                picked = jnp.concatenate(
                    [result[low:low + rows // 2], result[low_extra:low_extra + extra // 2]], axis=0
                )
                ordered = jnp.dot(order[...], picked, preferred_element_type=F32).astype(BF16)
                staged[k % 2, side * half:(side + 1) * half, pl.ds(start, UNITS)] = ordered
            return carry

        lax.fori_loop(0, n_units // UNITS, unit_body, 0)
        out_copy(k).start()

    def step(i, carry):
        @pl.when((i >= 1) & (i < n_z))
        def _():
            z_copy(i).wait_recv()

        @pl.when(i < n_z)
        def _():
            x_copy(i, 0).start()
            x_copy(i, 1).start()
            d_copy(i, 0, core).start()

        @pl.when((i >= 1) & (i < n_z + 1))
        def _():
            k = i - 1
            for way in range(2):
                x_arrival(k, way).wait_recv()
                f_copy(k, way).start()
                d_copy(k, 1 + way, core).start()

        @pl.when(i >= 2)
        def _():
            k = i - 2
            for way in range(2):
                f_arrival(k, way).wait_recv()
                d_copy(k, 3 + way, core).start()
            for piece in range(5):
                d_copy(k, piece, 1 - core).wait_recv()
            multiply(k)

        return carry

    lax.fori_loop(0, n_z + 2, step, 0)

    hidden_max = jnp.max(jnp.max(hidden_peak[...], axis=0, keepdims=True), axis=1, keepdims=True) / own_in
    hidden_rows = jnp.where(iota((n_z, 128), 0) == z, hidden_max, 0.0)
    current = jnp.concatenate([grad_peak[...], hidden_rows], axis=0)
    base = 0
    for turn, phase in enumerate(peers):
        message[turn] = current
        for j, peer in enumerate(phase):
            remote(message.at[turn], inbox.at[base + j], m_send.at[base + j], m_recv.at[base + j], peer).start()
        for j, peer in enumerate(phase):
            remote(message.at[turn], inbox.at[base + j], m_send.at[base + j], m_recv.at[base + j], peer).wait_recv()
            current = jnp.maximum(current, inbox[base + j])
        base += len(phase)

    def history(old, peaks):
        diagonal = jnp.where(iota((n_z, 128), 0) == iota((n_z, 128), 1), peaks, 0.0)
        newest = jnp.max(diagonal, axis=0, keepdims=True)[:, 0:n_z]
        return jnp.concatenate([old[1:], newest], axis=0)

    new_grad[...] = history(hist_grad[...], current[0:n_z])
    new_hidden[...] = history(hist_hidden[...], current[n_z:2 * n_z])

    out_copy(n_z - 2).wait()
    out_copy(n_z - 1).wait()

    def drain(k, carry):
        @pl.when(k >= 1)
        def _():
            z_copy(k).wait_send()

        for way in range(2):
            x_copy(k, way).wait_send()
            f_copy(k, way).wait_send()
        for piece in range(5):
            d_copy(k, piece, core).wait_send()
        return carry

    lax.fori_loop(0, n_z, drain, 0)
    base = 0
    for turn, phase in enumerate(peers):
        for j, peer in enumerate(phase):
            remote(message.at[turn], inbox.at[base + j], m_send.at[base + j], m_recv.at[base + j], peer).wait_send()
        base += len(phase)


def solution(mesh):
    n_y = mesh.shape["dp"]
    n_expert = mesh.shape["expert"]

    def per_device(grad_out, expert_ids, down_weight, history_grad, history_hidden):
        tok, features = grad_out.shape
        n_z = history_grad.shape[1]
        members = n_expert // n_z
        n_x = members // CORES
        units = down_weight.shape[1]
        capacity = tok * 9 // 32
        tail = capacity - MAIN
        width = features * tail // MAIN
        rows, extra = members * MAIN, members * tail
        n_messages = members - 1 + n_y - 1 + n_z - 1
        dma = pltpu.SemaphoreType.DMA
        vmem, anywhere = pl.BlockSpec(memory_space=pltpu.VMEM), pl.BlockSpec(memory_space=pl.ANY)
        small = jax.ShapeDtypeStruct(history_grad.shape, F32)
        return pl.pallas_call(
            functools.partial(kernel, n_y, n_z, n_x, capacity),
            out_shape=(jax.ShapeDtypeStruct((1, 1, n_expert * capacity, units), BF16), small, small),
            in_specs=[vmem, vmem, vmem, anywhere, anywhere],
            out_specs=(anywhere, vmem, vmem),
            scratch_shapes=[
                pltpu.VMEM((tok, features), BF16),
                pltpu.VMEM((units, features), BF16),
                pltpu.VMEM((n_z, MAIN, features + width), BF16),
                pltpu.VMEM((n_z, rows + extra, features + width), BF16),
                pltpu.VMEM((2, members * capacity, units), BF16),
                pltpu.VMEM((n_z, tok), F32),
                pltpu.VMEM((rows, rows), BF16),
                pltpu.VMEM((members * capacity // 2, members * capacity // 2), BF16),
                pltpu.VMEM((n_z, 128), F32),
                pltpu.VMEM((8, UNITS), F32),
                pltpu.VMEM((3, 2 * n_z, 128), F32),
                pltpu.VMEM((n_messages, 2 * n_z, 128), F32),
                dma((2,)), dma((2,)),
                dma((n_z,)), dma((n_z,)),
                dma((n_z, 2)), dma((n_z, 2)),
                dma((n_z, 2)), dma((n_z, 2)),
                dma((n_z, 5)), dma((n_z, 5)),
                dma((n_messages,)), dma((n_messages,)),
            ],
            compiler_params=pltpu.CompilerParams(
                collective_id=0, has_side_effects=True, vmem_limit_bytes=60 * 1024 * 1024
            ),
        )(expert_ids.T, history_grad, history_hidden, grad_out, down_weight[0])

    both = ("dp", "expert")
    return jax.shard_map(
        per_device,
        mesh=mesh,
        in_specs=(P(both, None), P(both, None), P("expert", None, None), P(), P()),
        out_specs=(P("dp", "expert", None, None), P(), P()),
        check_vma=False,
    )
```

time: 403 us -> 102 us (0.25)
  waiting for transfers between devices: 224 us -> 0 us
  blocking collectives: 99.9 us -> 0 us
  Pallas kernels: 0 us -> 95 us
  other arithmetic: 24.5 us -> 0 us
  matrix products: 22.7 us -> 0 us
  local copies, waits for them, and re-layouts: 24.8 us -> 6.22 us
  starting transfers between devices: 5.83 us -> 0 us
    ppermute x3 -> x0, waiting for transfers between devices: 224 us -> none  [from_partner(): lax.ppermute(shard, axis, [(i, i ^ 1 << apart) for i in range(lax.axis_si...]
    pallas_call x0 -> x1, Pallas kernels: none -> 95 us  [per_device(): pl.pallas_call(functools.partial(kernel, n_y, n_z, n_x, capacity), out_sh...]
    all_to_all x1 -> x0, blocking collectives: 59.8 us -> none  [per_device(): lax.all_to_all(pieces, EXPERT, split_axis=0, concat_axis=0, tiled=True)]
    pmax x4 -> x0, blocking collectives: 40.1 us -> none  [by_axis(): return functools.reduce(lax.pmax, axes, shard)]
    dot_general x2 -> x0, matrix products: 22.7 us -> none  [the longest x1 20.9 us: per_device(): jnp.einsum('jsic,ujc->siu', collected, weight_parts, preferred_element_ty...]
    select_n x4 -> x0, other arithmetic: 14.3 us -> none  [the longest x3 13.6 us: per_device(): first = jnp.where(upper, partner, collected)]
    reshape x1 -> x0, local copies, waits for them, and re-layouts: 7.19 us -> none  [per_device(): hidden_scaled = scaled.reshape(1, 1, -1, scaled.shape[2])]
    concatenate x3 -> x0, other arithmetic: 6.76 us -> none  [the longest x2 6.15 us: per_device(): collected = jnp.concatenate([first, second], axis=0)]
  transfers between devices with their start and end apart: 3 -> 0, of which waited for: 3 -> 0; matrix products, arithmetic and copies ran while one was open for 2% -> 0% of each run, Pallas kernels for 0% -> 0%
where the time goes in v1:
time: 102 us
  Pallas kernels  95 us (93%)
  local copies, waits for them, and re-layouts  6.22 us (6%)
    pallas_call x1, Pallas kernels, per_device(): pl.pallas_call(functools.partial(kernel, n_y, n_z, n_x, capacity), out_sh...  95 us
    unnamed x7, local copies, waits for them, and re-layouts  6.22 us

profile of v1, /device:TPU:1, one launch (start us, length us, event | category | flops | bytes accessed | tf_op | source)
XLA Modules:
  0.0 101.8 jit_solution(4160876502093645163)
XLA Ops:
  0.6 95.0 %shard_map.76 = (bf16[1,1,2304,1024]{3,2,1,0:T(8,128)(2,1)}, f32[8,8]{1,0:T(8,128)}, f32[8,8]{1,0:T(8,128)}) custom-call(s32[2,128]{1,0:T(2,128)} %bitcast.3, f32[8,8]{1,0:T(8,128)} %hist_grad.1, f32[8,8]{1,0:T(8,128)} %hist_hidden.1, bf16[128,3072]{1,0:T(8,128)(2,1)} %grad_hbm.1, bf16[1024,3072]{1,0:T(8,128)(2,1)} %bitcast.2), custom_call_target="tpu_custom_call" | custom-call | tf_op jit(solution)/shard_map/pallas_call | solution.py:306
  95.6 0.0 copy-start.1
  95.6 0.0 copy-start
  95.6 5.0 %copy.11 = bf16[1,1,2304,1024]{3,2,1,0:T(8,128)(2,1)} copy(bf16[1,1,2304,1024]{3,2,1,0:T(8,128)(2,1)} %get-tuple-element.6) | data formatting | bytes 9437184
  100.7 0.0 copy-done.1
  100.7 0.6 copy.12
  101.3 0.0 copy-done
  101.3 0.6 copy.13
Async XLA Ops:
  95.6 5.1 %copy-start.1 = (f32[8,8]{1,0:T(8,128)S(1)}, f32[8,8]{1,0:T(8,128)}, u32[]{:S(2)}) copy-start(f32[8,8]{1,0:T(8,128)} %get-tuple-element.7) | copy-start | bytes 772
  95.6 5.6 %copy-start = (f32[8,8]{1,0:T(8,128)S(1)}, f32[8,8]{1,0:T(8,128)}, u32[]{:S(2)}) copy-start(f32[8,8]{1,0:T(8,128)} %get-tuple-element.8) | copy-start | bytes 772

commit v2 on v1

v2 whole, which is shorter than its diff:
```python
import functools

import jax
import jax.numpy as jnp
from jax import lax
from jax.experimental import pallas as pl
from jax.experimental.pallas import tpu as pltpu
from jax.sharding import PartitionSpec as P

MESH = pl.DeviceIdType.MESH
F32, BF16 = jnp.float32, jnp.bfloat16
CORES = 2
MAIN = 32
HALF = MAIN // 2
PAIR = CORES * MAIN
NEAR = 3 * PAIR
FAR = NEAR + 32
FAR_ROWS = PAIR + 16


def iota(shape, axis):
    return lax.broadcasted_iota(jnp.int32, shape, axis)


def unfold_matrix(rows, tail, fold):
    extra = rows // MAIN * tail
    goes, comes = iota((rows, rows), 0), iota((rows, rows), 1)
    part = functools.reduce(lambda a, b: a + b, [(goes >= extra * i).astype(jnp.int32) for i in range(1, fold)])
    rest = goes - part * extra
    wanted = rest // tail * MAIN + part * tail + rest % tail
    return (wanted == comes).astype(F32).astype(BF16)


def kernel(
    n_y, n_z, n_x, capacity,
    ids_hbm, hist_grad_hbm, hist_hidden_hbm, grad_hbm, weight_hbm,
    out_ref, new_grad, new_hidden,
    ids_ref, hist_grad, hist_hidden, grad_v, weight_v, queue, gathered, slot_of, unfold_near, unfold_far, peaks, hidden_peak, message, inbox,
    local_sem, z_send, z_recv, x_send, x_recv, f_send, f_recv, d_send, d_recv, m_send, m_recv,
):
    tok, features = grad_v.shape
    units = weight_v.shape[0]
    tail = capacity - MAIN
    fold = MAIN // tail
    width = features // fold
    members = n_x * CORES

    y = lax.axis_index("dp")
    me = lax.axis_index("expert")
    core = me % CORES
    x = (me // CORES) % n_x
    z = me // members
    group = me % members

    def at(to_z, to_x, to_core):
        return (y, (to_z * n_x + to_x) * CORES + to_core)

    right, left, far = (x + 1) % n_x, (x + n_x - 1) % n_x, (x + 2) % n_x
    partner = at(z, x, 1 - core)
    sides = (at(z, right, core), at(z, left, core))

    peers = [
        [
            ((y + i) % n_y, z * members + (group + j) % members)
            for i in range(n_y) for j in range(members) if i + j > 0
        ],
        [at((z + j) % n_z, x, core) for j in range(1, n_z)],
    ]
    barrier = pltpu.get_barrier_semaphore()
    for phase in peers[::-1]:
        for peer in phase:
            pl.semaphore_signal(barrier, inc=1, device_id=peer, device_id_type=MESH)

    pairs = (ids_hbm, ids_ref), (hist_grad_hbm, hist_grad), (hist_hidden_hbm, hist_hidden), (grad_hbm, grad_v), (weight_hbm, weight_v)
    loads = [pltpu.make_async_copy(source, target, local_sem.at[i]) for i, (source, target) in enumerate(pairs)]
    for load in loads:
        load.start()
    grad_in, weight_in = loads[3:]
    for load in loads[:3]:
        load.wait()

    ids = ids_ref[...]
    named = (iota((n_z, tok), 0) == ids[0:1, :]) | (iota((n_z, tok), 0) == ids[1:2, :])
    earlier = (iota((tok, tok), 0) < iota((tok, tok), 1)).astype(F32).astype(BF16)
    before = jnp.dot(named.astype(F32).astype(BF16), earlier, preferred_element_type=F32)
    slot_of[...] = jnp.where(named, before, -1.0)

    scale_in = 1.0 / jnp.max(hist_grad[...], axis=0, keepdims=True)
    scale_hidden = 1.0 / jnp.max(hist_hidden[...], axis=0, keepdims=True)
    own = iota((1, n_z), 1) == z
    own_in = jnp.sum(jnp.where(own, scale_in, 0.0), axis=1, keepdims=True)
    own_hidden = jnp.sum(jnp.where(own, scale_hidden, 0.0), axis=1, keepdims=True)
    factor = own_hidden / own_in

    all_rows = n_z * MAIN
    slots = jnp.broadcast_to(slot_of[...][:, None, :], (n_z, MAIN, tok)).reshape(all_rows, tok)
    in_block = iota((all_rows, tok), 0) % MAIN
    pick_main = (slots == in_block.astype(F32)).astype(F32).astype(BF16)
    is_tail = slots == (in_block % tail + MAIN).astype(F32)
    row_scale = jnp.sum(
        jnp.where(iota((all_rows, n_z), 1) == iota((all_rows, n_z), 0) // MAIN, scale_in, 0.0), axis=1, keepdims=True
    )

    def scaled(values):
        return jnp.clip(values * row_scale, -1.0, 1.0).astype(BF16).reshape(n_z, MAIN, width)

    def folded_peak(values):
        return functools.reduce(jnp.maximum, [jnp.abs(values[:, i:i + 128]) for i in range(0, width, 128)])

    grad_in.wait()
    tails = jnp.zeros((all_rows, width), F32)
    peak = jnp.zeros((all_rows, 128), F32)
    for part in range(fold):
        piece = grad_v[:, part * width:(part + 1) * width]
        values = jnp.dot(pick_main, piece, preferred_element_type=F32)
        queue[:, :, part * width:(part + 1) * width] = scaled(values)
        peak = jnp.maximum(peak, folded_peak(values))
        pick = (is_tail & (in_block // tail == part)).astype(F32).astype(BF16)
        tails = tails + jnp.dot(pick, piece, preferred_element_type=F32)
    queue[:, :, features:] = scaled(tails)
    peak = jnp.maximum(peak, folded_peak(tails))
    peak = jnp.max(jnp.max(peak.reshape(n_z, MAIN, 128), axis=1), axis=1, keepdims=True)
    diagonal = jnp.where(iota((n_z, 128), 0) == iota((n_z, 128), 1), peak, 0.0)
    peaks[...] = jnp.max(diagonal, axis=0, keepdims=True)
    hidden_peak[...] = jnp.zeros_like(hidden_peak)
    gathered[0, pl.ds(pl.multiple_of(core * MAIN, MAIN), MAIN), :] = queue[z]
    unfold_near[...] = unfold_matrix(NEAR, tail, fold)
    unfold_far[...] = unfold_matrix(PAIR, tail, fold)

    pl.semaphore_wait(barrier, sum(len(phase) for phase in peers))

    starts = (0, PAIR, 2 * PAIR, FAR)

    def offset(k):
        return ((k + 1) // 2) * (2 * (k % 2) - 1)

    def part_of(k, place, whose, low=0, count=MAIN):
        start = pl.multiple_of(starts[place] + whose * MAIN + low, HALF)
        return gathered.at[k, pl.ds(start, count), :]

    def remote(source, target, send, recv, device):
        return pltpu.make_async_remote_copy(
            src_ref=source, dst_ref=target, send_sem=send, recv_sem=recv, device_id=device, device_id_type=MESH
        )

    def z_copy(k):
        to_z = (z - offset(k) + n_z) % n_z
        return remote(queue.at[to_z], part_of(k, 0, core), z_send.at[k], z_recv.at[k], at(to_z, x, core))

    def x_copy(k, way):
        return remote(
            part_of(k, 0, core), part_of(k, 1 + way, core), x_send.at[k, way], x_recv.at[k, way], sides[way]
        )

    def f_copy(k, way):
        return remote(
            part_of(k, 1 + way, core, way * HALF, HALF), part_of(k, 3, core, way * HALF, HALF),
            f_send.at[k, way], f_recv.at[k, way], sides[way],
        )

    def d_copy(k, piece, whose):
        if piece < 3:
            block = part_of(k, piece, whose)
        else:
            block = part_of(k, 3, whose, (piece - 3) * HALF, HALF)
        return remote(block, block, d_send.at[k, piece], d_recv.at[k, piece], partner)

    def pass_far(k):
        for way in range(2):
            f_copy(k, way).wait_recv()
            d_copy(k, 3 + way, core).start()

    def place_tails(k, low, rows, unfold):
        extra = rows // MAIN * tail
        room = -(-extra // 16) * 16
        folded = gathered[k, low:low + rows, features:features + width]
        plain = jnp.dot(unfold[...], folded, preferred_element_type=F32)
        for part in range(fold):
            piece = plain[part * extra:(part + 1) * extra]
            piece = jnp.concatenate([piece, jnp.zeros((room - extra, width), F32)], axis=0).astype(BF16)
            gathered[k, low + rows:low + rows + room, part * width:(part + 1) * width] = piece

    def multiply(k, low, rows, places, first, count):
        product = lax.dot_general(
            gathered[k, low:low + rows, 0:features], weight_v[first:first + count, :],
            (((1,), (1,)), ((), ())), preferred_element_type=F32,
        )
        size = jnp.max(jnp.abs(product).reshape(rows // 8, 8, count), axis=0)
        size = functools.reduce(jnp.maximum, [size[:, i:i + 128] for i in range(0, count, 128)])
        hidden_peak[...] = jnp.maximum(hidden_peak[...], size)
        result = jnp.clip(product * factor, -1.0, 1.0)
        from_z = (z + offset(k) + n_z) % n_z
        for place in places:
            start = starts[place] - low
            last = (NEAR + place * CORES * tail if place < 3 else FAR + PAIR) - low
            pieces = []
            for member in range(CORES):
                pieces.append(result[start + member * MAIN:start + (member + 1) * MAIN])
                pieces.append(result[last + member * tail:last + (member + 1) * tail])
            ordered = jnp.concatenate(pieces, axis=0).astype(BF16)
            out_ref[from_z * n_x + (x, left, right, far)[place], :, first:first + count] = ordered

    def near_ready(k):
        for piece in range(3):
            d_copy(k, piece, 1 - core).wait_recv()
        place_tails(k, 0, NEAR, unfold_near)

    def far_ready(k):
        for piece in range(3, 5):
            d_copy(k, piece, 1 - core).wait_recv()
        place_tails(k, FAR, PAIR, unfold_far)

    def send_own(k):
        x_copy(k, 0).start()
        x_copy(k, 1).start()
        d_copy(k, 0, core).start()

    def z_body(k, carry):
        z_copy(k).start()
        return carry

    send_own(0)
    lax.fori_loop(1, n_z, z_body, 0)
    weight_in.wait()

    last = n_z - 1

    def step(i, carry):
        @pl.when(i < last)
        def _():
            z_copy(i + 1).wait_recv()
            send_own(i + 1)

        @pl.when(i >= 2)
        def _():
            k = i - 2
            pass_far(k)
            near_ready(k)
            far_ready(k)
            multiply(k, 0, FAR + FAR_ROWS, (0, 1, 2, 3), 0, units)

        for way in range(2):
            x_copy(i, way).wait_recv()
            f_copy(i, way).start()
            d_copy(i, 1 + way, core).start()
        return carry

    lax.fori_loop(0, n_z, step, 0)
    near_ready(last)
    multiply(last, 0, FAR, (0, 1, 2), 0, units // 2)
    pass_far(last - 1)
    multiply(last, 0, FAR, (0, 1, 2), units // 2, units // 2)
    near_ready(last - 1)
    far_ready(last - 1)
    multiply(last - 1, 0, FAR + FAR_ROWS, (0, 1, 2, 3), 0, units // 2)
    pass_far(last)
    multiply(last - 1, 0, FAR + FAR_ROWS, (0, 1, 2, 3), units // 2, units // 2)
    far_ready(last)
    multiply(last, FAR, FAR_ROWS, (3,), 0, units)

    hidden_max = jnp.max(jnp.max(hidden_peak[...], axis=0, keepdims=True), axis=1, keepdims=True) / own_in
    hidden_row = jnp.where(iota((1, 128), 1) == z, hidden_max, 0.0)
    current = jnp.where(iota((2, 128), 0) == 0, peaks[...], hidden_row)
    base = 0
    for turn, phase in enumerate(peers):
        message[turn] = current
        for j, peer in enumerate(phase):
            remote(message.at[turn], inbox.at[base + j], m_send.at[base + j], m_recv.at[base + j], peer).start()
        for j, peer in enumerate(phase):
            remote(message.at[turn], inbox.at[base + j], m_send.at[base + j], m_recv.at[base + j], peer).wait_recv()
            current = jnp.maximum(current, inbox[base + j])
        base += len(phase)

    new_grad[...] = jnp.concatenate([hist_grad[...][1:], current[0:1, 0:n_z]], axis=0)
    new_hidden[...] = jnp.concatenate([hist_hidden[...][1:], current[1:2, 0:n_z]], axis=0)

    def drain(k, carry):
        @pl.when(k >= 1)
        def _():
            z_copy(k).wait_send()

        for way in range(2):
            x_copy(k, way).wait_send()
            f_copy(k, way).wait_send()
        for piece in range(5):
            d_copy(k, piece, core).wait_send()
        return carry

    lax.fori_loop(0, n_z, drain, 0)
    base = 0
    for turn, phase in enumerate(peers):
        for j, peer in enumerate(phase):
            remote(message.at[turn], inbox.at[base + j], m_send.at[base + j], m_recv.at[base + j], peer).wait_send()
        base += len(phase)


def solution(mesh):
    n_y = mesh.shape["dp"]
    n_expert = mesh.shape["expert"]

    def per_device(grad_out, expert_ids, down_weight, history_grad, history_hidden):
        tok, features = grad_out.shape
        n_z = history_grad.shape[1]
        members = n_expert // n_z
        n_x = members // CORES
        units = down_weight.shape[1]
        capacity = tok * 9 // 32
        width = features * (capacity - MAIN) // MAIN
        n_messages = n_y * members - 1 + n_z - 1
        dma = pltpu.SemaphoreType.DMA
        vmem, hbm = pl.BlockSpec(memory_space=pltpu.VMEM), pl.BlockSpec(memory_space=pltpu.HBM)
        small = jax.ShapeDtypeStruct(history_grad.shape, F32)
        arguments = expert_ids.T, history_grad, history_hidden, grad_out, down_weight[0]
        rows, new_grad, new_hidden = pl.pallas_call(
            functools.partial(kernel, n_y, n_z, n_x, capacity),
            out_shape=(jax.ShapeDtypeStruct((n_expert // CORES, CORES * capacity, units), BF16), small, small),
            in_specs=[hbm] * 5,
            out_specs=(vmem, vmem, vmem),
            scratch_shapes=[
                pltpu.VMEM((2, tok), jnp.int32),
                pltpu.VMEM(history_grad.shape, F32),
                pltpu.VMEM(history_grad.shape, F32),
                pltpu.VMEM((tok, features), BF16),
                pltpu.VMEM((units, features), BF16),
                pltpu.VMEM((n_z, MAIN, features + width), BF16),
                pltpu.VMEM((n_z, FAR + FAR_ROWS, features + width), BF16),
                pltpu.VMEM((n_z, tok), F32),
                pltpu.VMEM((NEAR, NEAR), BF16),
                pltpu.VMEM((PAIR, PAIR), BF16),
                pltpu.VMEM((1, 128), F32),
                pltpu.VMEM((8, 128), F32),
                pltpu.VMEM((2, 2, 128), F32),
                pltpu.VMEM((n_messages, 2, 128), F32),
                dma((5,)),
                dma((n_z,)), dma((n_z,)),
                dma((n_z, 2)), dma((n_z, 2)),
                dma((n_z, 2)), dma((n_z, 2)),
                dma((n_z, 5)), dma((n_z, 5)),
                dma((n_messages,)), dma((n_messages,)),
            ],
            compiler_params=pltpu.CompilerParams(
                collective_id=0, has_side_effects=True, vmem_limit_bytes=46 * 1024 * 1024
            ),
        )(*(pltpu.with_memory_space_constraint(a, pltpu.HBM) for a in arguments))
        return rows.reshape(1, 1, n_expert * capacity, units), new_grad, new_hidden

    both = ("dp", "expert")
    return jax.shard_map(
        per_device,
        mesh=mesh,
        in_specs=(P(both, None), P(both, None), P("expert", None, None), P(), P()),
        out_specs=(P("dp", "expert", None, None), P(), P()),
        check_vma=False,
    )
```

time: 102 us -> 91.7 us (0.90)
  Pallas kernels: 95 us -> 87.6 us
  local copies, waits for them, and re-layouts: 6.22 us -> 3.37 us
    pallas_call x1, Pallas kernels: 95 us -> 87.6 us  [per_device(): pl.pallas_call(functools.partial(kernel, n_y, n_z, n_x, capacity), out_sh...]
    unnamed x7 -> x3, local copies, waits for them, and re-layouts: 6.22 us -> 3.37 us
where the time goes in v2:
time: 91.7 us; the launch traced here: 91.6 us
  Pallas kernels  87.6 us (96%)
  local copies, waits for them, and re-layouts  3.37 us (4%)
    pallas_call x1, Pallas kernels, per_device(): pl.pallas_call(functools.partial(kernel, n_y, n_z, n_x, capacity), out_sh...  87.6 us
    unnamed x3, local copies, waits for them, and re-layouts  3.37 us

profile of v2, /device:TPU:1, one launch (start us, length us, event | category | flops | bytes accessed | tf_op | source)
XLA Modules:
  0.0 91.6 jit_solution(6861571313920606644)
XLA Ops:
  0.6 87.6 %shard_map.76 = (bf16[32,72,1024]{2,1,0:T(8,128)(2,1)S(1)}, f32[8,8]{1,0:T(8,128)S(1)}, f32[8,8]{1,0:T(8,128)S(1)}) custom-call(s32[2,128]{1,0:T(2,128)} %bitcast.5, f32[8,8]{1,0:T(8,128)} %hist_grad_hbm.1, f32[8,8]{1,0:T(8,128)} %hist_hidden_hbm.1, bf16[128,3072]{1,0:T(8,128)(2,1)} %grad_hbm.1, bf16[1024,3072]{1,0:T(8,128)(2,1)} %bitcast.4), custom_call_target="tpu_custom_call" | custom-call | tf_op jit(solution)/shard_map/pallas_call | solution.py:314
  88.2 2.2 %copy.11 = bf16[1,1,2304,1024]{3,2,1,0:T(8,128)(2,1)} copy(bf16[1,1,2304,1024]{3,2,1,0:T(8,128)(2,1)S(1)} %bitcast.3) | data formatting | bytes 9437184
  90.4 0.6 copy.12
  91.0 0.6 copy.13

commit v3 on v2

--- a/solution.py
+++ b/solution.py
@@ -16,6 +16,7 @@
 NEAR = 3 * PAIR
 FAR = NEAR + 32
 FAR_ROWS = PAIR + 16
+PIECES = 8
 
 
 def iota(shape, axis):
@@ -36,7 +37,7 @@
     ids_hbm, hist_grad_hbm, hist_hidden_hbm, grad_hbm, weight_hbm,
     out_ref, new_grad, new_hidden,
     ids_ref, hist_grad, hist_hidden, grad_v, weight_v, queue, gathered, slot_of, unfold_near, unfold_far, peaks, hidden_peak, message, inbox,
-    local_sem, z_send, z_recv, x_send, x_recv, f_send, f_recv, d_send, d_recv, m_send, m_recv,
+    local_sem, z_send, z_recv, o_send, o_recv, x_send, x_recv, f_send, f_recv, d_send, d_recv, m_send, m_recv,
 ):
     tok, features = grad_v.shape
     units = weight_v.shape[0]
@@ -152,6 +153,13 @@
             part_of(k, 0, core), part_of(k, 1 + way, core), x_send.at[k, way], x_recv.at[k, way], sides[way]
         )
 
+    def first_copy(way, late):
+        low = HALF * (way ^ late)
+        return remote(
+            part_of(0, 0, core, low, HALF), part_of(0, 1 + way, core, low, HALF),
+            o_send.at[way, late], o_recv.at[way, late], sides[way],
+        )
+
     def f_copy(k, way):
         return remote(
             part_of(k, 1 + way, core, way * HALF, HALF), part_of(k, 3, core, way * HALF, HALF),
@@ -219,8 +227,11 @@
         z_copy(k).start()
         return carry
 
-    send_own(0)
+    for late in range(2):
+        for way in range(2):
+            first_copy(way, late).start()
     lax.fori_loop(1, n_z, z_body, 0)
+    d_copy(0, 0, core).start()
     weight_in.wait()
 
     last = n_z - 1
@@ -245,7 +256,15 @@
             d_copy(i, 1 + way, core).start()
         return carry
 
-    lax.fori_loop(0, n_z, step, 0)
+    for way in range(2):
+        first_copy(way, 0).wait_recv()
+        f_copy(0, way).start()
+    z_copy(1).wait_recv()
+    send_own(1)
+    for way in range(2):
+        first_copy(way, 1).wait_recv()
+        d_copy(0, 1 + way, core).start()
+    lax.fori_loop(1, n_z, step, 0)
     near_ready(last)
     multiply(last, 0, FAR, (0, 1, 2), 0, units // 2)
     pass_far(last - 1)
@@ -278,20 +297,40 @@
         @pl.when(k >= 1)
         def _():
             z_copy(k).wait_send()
+            x_copy(k, 0).wait_send()
+            x_copy(k, 1).wait_send()
 
         for way in range(2):
-            x_copy(k, way).wait_send()
             f_copy(k, way).wait_send()
         for piece in range(5):
             d_copy(k, piece, core).wait_send()
         return carry
 
+    for way in range(2):
+        for late in range(2):
+            first_copy(way, late).wait_send()
     lax.fori_loop(0, n_z, drain, 0)
     base = 0
     for turn, phase in enumerate(peers):
         for j, peer in enumerate(phase):
             remote(message.at[turn], inbox.at[base + j], m_send.at[base + j], m_recv.at[base + j], peer).wait_send()
         base += len(phase)
+
+
+def write_out(*refs):
+    count = len(refs) // 2
+    sems = refs[-1]
+    copies = []
+    for i in range(3):
+        cuts = PIECES if i == 0 else 1
+        size = refs[i].shape[0] // cuts
+        for j in range(cuts):
+            source, target = (ref.at[pl.ds(j * size, size)] for ref in (refs[i], refs[count + i]))
+            copies.append(pltpu.make_async_copy(source, target, sems.at[len(copies)]))
+    for copy in copies:
+        copy.start()
+    for copy in copies:
+        copy.wait()
 
 
 def solution(mesh):
@@ -308,10 +347,11 @@
         width = features * (capacity - MAIN) // MAIN
         n_messages = n_y * members - 1 + n_z - 1
         dma = pltpu.SemaphoreType.DMA
+        anywhere = pl.BlockSpec(memory_space=pl.ANY)
         vmem, hbm = pl.BlockSpec(memory_space=pltpu.VMEM), pl.BlockSpec(memory_space=pltpu.HBM)
         small = jax.ShapeDtypeStruct(history_grad.shape, F32)
         arguments = expert_ids.T, history_grad, history_hidden, grad_out, down_weight[0]
-        rows, new_grad, new_hidden = pl.pallas_call(
+        results = pl.pallas_call(
             functools.partial(kernel, n_y, n_z, n_x, capacity),
             out_shape=(jax.ShapeDtypeStruct((n_expert // CORES, CORES * capacity, units), BF16), small, small),
             in_specs=[hbm] * 5,
@@ -333,6 +373,7 @@
                 pltpu.VMEM((n_messages, 2, 128), F32),
                 dma((5,)),
                 dma((n_z,)), dma((n_z,)),
+                dma((2, 2)), dma((2, 2)),
                 dma((n_z, 2)), dma((n_z, 2)),
                 dma((n_z, 2)), dma((n_z, 2)),
                 dma((n_z, 5)), dma((n_z, 5)),
@@ -342,6 +383,14 @@
                 collective_id=0, has_side_effects=True, vmem_limit_bytes=46 * 1024 * 1024
             ),
         )(*(pltpu.with_memory_space_constraint(a, pltpu.HBM) for a in arguments))
+        rows, new_grad, new_hidden = pl.pallas_call(
+            write_out,
+            out_shape=tuple(jax.ShapeDtypeStruct(a.shape, a.dtype) for a in results),
+            in_specs=[anywhere] * 3,
+            out_specs=(hbm,) * 3,
+            scratch_shapes=[dma((PIECES + 2,))],
+            compiler_params=pltpu.CompilerParams(vmem_limit_bytes=1024 * 1024),
+        )(*results)
         return rows.reshape(1, 1, n_expert * capacity, units), new_grad, new_hidden
 
     both = ("dp", "expert")

time: 91.7 us -> 90.5 us (0.987)
  local copies, waits for them, and re-layouts: 3.37 us -> 0 us
  Pallas kernels: 87.6 us -> 89.8 us
    unnamed x3 -> x0, local copies, waits for them, and re-layouts: 3.37 us -> none
    pallas_call x0 -> x1, Pallas kernels: none -> 2.27 us  [per_device(): pl.pallas_call(write_out, out_shape=tuple((jax.ShapeDtypeStruct(a.shape,...]
where the time goes in v3:
time: 90.5 us; the launch traced here: 90.4 us
  Pallas kernels  89.8 us (99%)
    pallas_call x1, Pallas kernels, per_device(): pl.pallas_call(functools.partial(kernel, n_y, n_z, n_x, capacity), out_sh...  87.5 us
    pallas_call x1, Pallas kernels, per_device(): pl.pallas_call(write_out, out_shape=tuple((jax.ShapeDtypeStruct(a.shape,...  2.27 us

profile of v3, /device:TPU:1, one launch (start us, length us, event | category | flops | bytes accessed | tf_op | source)
XLA Modules:
  0.0 90.4 jit_solution(7773350103585056612)
XLA Ops:
  0.6 87.5 %shard_map.76 = (bf16[32,72,1024]{2,1,0:T(8,128)(2,1)S(1)}, f32[8,8]{1,0:T(8,128)S(1)}, f32[8,8]{1,0:T(8,128)S(1)}) custom-call(s32[2,128]{1,0:T(2,128)} %bitcast.4, f32[8,8]{1,0:T(8,128)} %hist_grad_hbm.1, f32[8,8]{1,0:T(8,128)} %hist_hidden_hbm.1, bf16[128,3072]{1,0:T(8,128)(2,1)} %grad_hbm.1, bf16[1024,3072]{1,0:T(8,128)(2,1)} %bitcast.3), custom_call_target="tpu_custom_call" | custom-call | tf_op jit(solution)/shard_map/pallas_call | solution.py:354
  88.2 2.3 %shard_map.77 = (bf16[32,72,1024]{2,1,0:T(8,128)(2,1)}, f32[8,8]{1,0:T(8,128)}, f32[8,8]{1,0:T(8,128)}) custom-call(bf16[32,72,1024]{2,1,0:T(8,128)(2,1)S(1)} %get-tuple-element.9.refs_0_, f32[8,8]{1,0:T(8,128)S(1)} %get-tuple-element.10.refs_1_, f32[8,8]{1,0:T(8,128)S(1)} %get-tuple-element.11.refs_2_), custom_call_target="tpu_custom_call" | custom-call | tf_op jit(solution)/shard_map/pallas_call | solution.py:386

commit v4 on v3

--- a/solution.py
+++ b/solution.py
@@ -16,6 +16,8 @@
 NEAR = 3 * PAIR
 FAR = NEAR + 32
 FAR_ROWS = PAIR + 16
+TURNED = 256
+EARLY = 5
 PIECES = 8
 
 
@@ -36,8 +38,8 @@
     n_y, n_z, n_x, capacity,
     ids_hbm, hist_grad_hbm, hist_hidden_hbm, grad_hbm, weight_hbm,
     out_ref, new_grad, new_hidden,
-    ids_ref, hist_grad, hist_hidden, grad_v, weight_v, queue, gathered, slot_of, unfold_near, unfold_far, peaks, hidden_peak, message, inbox,
-    local_sem, z_send, z_recv, o_send, o_recv, x_send, x_recv, f_send, f_recv, d_send, d_recv, m_send, m_recv,
+    ids_ref, hist_grad, hist_hidden, grad_v, weight_v, weight_t, queue, gathered, slot_of, unfold_near, unfold_far, peaks, hidden_peak, message, inbox,
+    local_sem, z_send, z_recv, o_send, o_recv, x_send, x_recv, f_send, f_recv, d_send, d_recv, m_send, m_recv, h_send,
 ):
     tok, features = grad_v.shape
     units = weight_v.shape[0]
@@ -65,6 +67,7 @@
             ((y + i) % n_y, z * members + (group + j) % members)
             for i in range(n_y) for j in range(members) if i + j > 0
         ],
+        [at((z + j) % n_z, x, 1 - core) for j in range(1, n_z)],
         [at((z + j) % n_z, x, core) for j in range(1, n_z)],
     ]
     barrier = pltpu.get_barrier_semaphore()
@@ -190,8 +193,8 @@
 
     def multiply(k, low, rows, places, first, count):
         product = lax.dot_general(
-            gathered[k, low:low + rows, 0:features], weight_v[first:first + count, :],
-            (((1,), (1,)), ((), ())), preferred_element_type=F32,
+            gathered[k, low:low + rows, 0:features], weight_t[:, first:first + count],
+            (((1,), (0,)), ((), ())), preferred_element_type=F32,
         )
         size = jnp.max(jnp.abs(product).reshape(rows // 8, 8, count), axis=0)
         size = functools.reduce(jnp.maximum, [size[:, i:i + 128] for i in range(0, count, 128)])
@@ -236,11 +239,23 @@
 
     last = n_z - 1
 
+    def transpose(block, carry):
+        start = pl.multiple_of(block * TURNED, TURNED)
+        weight_t[pl.ds(start, TURNED), :] = weight_v[:, pl.ds(start, TURNED)].T
+        return carry
+
+    blocks = features // TURNED
+    early = blocks * EARLY // 12
+
     def step(i, carry):
         @pl.when(i < last)
         def _():
             z_copy(i + 1).wait_recv()
             send_own(i + 1)
+
+        @pl.when(i == 1)
+        def _():
+            lax.fori_loop(early, blocks, transpose, 0)
 
         @pl.when(i >= 2)
         def _():
@@ -256,6 +271,7 @@
             d_copy(i, 1 + way, core).start()
         return carry
 
+    lax.fori_loop(0, early, transpose, 0)
     for way in range(2):
         first_copy(way, 0).wait_recv()
         f_copy(0, way).start()
@@ -280,15 +296,41 @@
     hidden_max = jnp.max(jnp.max(hidden_peak[...], axis=0, keepdims=True), axis=1, keepdims=True) / own_in
     hidden_row = jnp.where(iota((1, 128), 1) == z, hidden_max, 0.0)
     current = jnp.where(iota((2, 128), 0) == 0, peaks[...], hidden_row)
-    base = 0
-    for turn, phase in enumerate(peers):
-        message[turn] = current
-        for j, peer in enumerate(phase):
-            remote(message.at[turn], inbox.at[base + j], m_send.at[base + j], m_recv.at[base + j], peer).start()
-        for j, peer in enumerate(phase):
-            remote(message.at[turn], inbox.at[base + j], m_send.at[base + j], m_recv.at[base + j], peer).wait_recv()
-            current = jnp.maximum(current, inbox[base + j])
-        base += len(phase)
+    def m_copy(turn, slot, peer):
+        return remote(message.at[turn], inbox.at[slot], m_send.at[slot], m_recv.at[slot], peer)
+
+    def to_hubs(act):
+        for slot, peer in enumerate(peers[0]):
+            pl.when((core + slot + 1) % CORES == 1)(functools.partial(act, m_copy(0, slot, peer)))
+
+    def hub_copy(place, slot, peer):
+        slot = len(peers[0]) + slot
+        return remote(message.at[1], inbox.at[slot], h_send.at[place], m_recv.at[slot], peer)
+
+    hub_copies = [hub_copy(to * (n_z - 1) + j, j, peers[1 + to][j]) for to in range(2) for j in range(n_z - 1)]
+    hub_copies.append(hub_copy(2 * (n_z - 1), n_z - 1, partner))
+    message[0] = current
+    to_hubs(lambda copy: copy.start())
+
+    @pl.when(core == 1)
+    def _():
+        total = message[0]
+        for slot, peer in enumerate(peers[0]):
+            m_copy(0, slot, peer).wait_recv()
+            total = jnp.maximum(total, inbox[slot])
+        message[1] = total
+        for copy in hub_copies:
+            copy.start()
+
+    @pl.when(core == 0)
+    def _():
+        hub_copies[-1].wait_recv()
+        message[1] = inbox[len(peers[0]) + n_z - 1]
+
+    current = message[1]
+    for j in range(n_z - 1):
+        hub_copies[j].wait_recv()
+        current = jnp.maximum(current, inbox[len(peers[0]) + j])
 
     new_grad[...] = jnp.concatenate([hist_grad[...][1:], current[0:1, 0:n_z]], axis=0)
     new_hidden[...] = jnp.concatenate([hist_hidden[...][1:], current[1:2, 0:n_z]], axis=0)
@@ -310,11 +352,12 @@
         for late in range(2):
             first_copy(way, late).wait_send()
     lax.fori_loop(0, n_z, drain, 0)
-    base = 0
-    for turn, phase in enumerate(peers):
-        for j, peer in enumerate(phase):
-            remote(message.at[turn], inbox.at[base + j], m_send.at[base + j], m_recv.at[base + j], peer).wait_send()
-        base += len(phase)
+    to_hubs(lambda copy: copy.wait_send())
+
+    @pl.when(core == 1)
+    def _():
+        for copy in hub_copies:
+            copy.wait_send()
 
 
 def write_out(*refs):
@@ -345,7 +388,7 @@
         units = down_weight.shape[1]
         capacity = tok * 9 // 32
         width = features * (capacity - MAIN) // MAIN
-        n_messages = n_y * members - 1 + n_z - 1
+        n_messages = n_y * members - 1 + n_z
         dma = pltpu.SemaphoreType.DMA
         anywhere = pl.BlockSpec(memory_space=pl.ANY)
         vmem, hbm = pl.BlockSpec(memory_space=pltpu.VMEM), pl.BlockSpec(memory_space=pltpu.HBM)
@@ -362,6 +405,7 @@
                 pltpu.VMEM(history_grad.shape, F32),
                 pltpu.VMEM((tok, features), BF16),
                 pltpu.VMEM((units, features), BF16),
+                pltpu.VMEM((features, units), BF16),
                 pltpu.VMEM((n_z, MAIN, features + width), BF16),
                 pltpu.VMEM((n_z, FAR + FAR_ROWS, features + width), BF16),
                 pltpu.VMEM((n_z, tok), F32),
@@ -377,7 +421,7 @@
                 dma((n_z, 2)), dma((n_z, 2)),
                 dma((n_z, 2)), dma((n_z, 2)),
                 dma((n_z, 5)), dma((n_z, 5)),
-                dma((n_messages,)), dma((n_messages,)),
+                dma((n_messages,)), dma((n_messages,)), dma((2 * n_z - 1,)),
             ],
             compiler_params=pltpu.CompilerParams(
                 collective_id=0, has_side_effects=True, vmem_limit_bytes=46 * 1024 * 1024

time: 90.5 us -> 89 us (0.983)
  Pallas kernels: 89.8 us -> 88.3 us
    pallas_call x1, Pallas kernels: 87.5 us -> 86 us  [per_device(): pl.pallas_call(functools.partial(kernel, n_y, n_z, n_x, capacity), out_sh...]
where the time goes in v4:
time: 89 us; the launch traced here: 88.9 us
  Pallas kernels  88.3 us (99%)
    pallas_call x1, Pallas kernels, per_device(): pl.pallas_call(functools.partial(kernel, n_y, n_z, n_x, capacity), out_sh...  86 us
    pallas_call x1, Pallas kernels, per_device(): pl.pallas_call(write_out, out_shape=tuple((jax.ShapeDtypeStruct(a.shape,...  2.27 us

profile of v4, /device:TPU:1, one launch (start us, length us, event | category | flops | bytes accessed | tf_op | source)
XLA Modules:
  0.0 88.9 jit_solution(13809770970410779021)
XLA Ops:
  0.6 86.0 %shard_map.76 = (bf16[32,72,1024]{2,1,0:T(8,128)(2,1)S(1)}, f32[8,8]{1,0:T(8,128)S(1)}, f32[8,8]{1,0:T(8,128)S(1)}) custom-call(s32[2,128]{1,0:T(2,128)} %bitcast.4, f32[8,8]{1,0:T(8,128)} %hist_grad_hbm.1, f32[8,8]{1,0:T(8,128)} %hist_hidden_hbm.1, bf16[128,3072]{1,0:T(8,128)(2,1)} %grad_hbm.1, bf16[1024,3072]{1,0:T(8,128)(2,1)} %bitcast.3), custom_call_target="tpu_custom_call" | custom-call | tf_op jit(solution)/shard_map/pallas_call | solution.py:397
  86.6 2.3 %shard_map.77 = (bf16[32,72,1024]{2,1,0:T(8,128)(2,1)}, f32[8,8]{1,0:T(8,128)}, f32[8,8]{1,0:T(8,128)}) custom-call(bf16[32,72,1024]{2,1,0:T(8,128)(2,1)S(1)} %get-tuple-element.9.refs_0_, f32[8,8]{1,0:T(8,128)S(1)} %get-tuple-element.10.refs_1_, f32[8,8]{1,0:T(8,128)S(1)} %get-tuple-element.11.refs_2_), custom_call_target="tpu_custom_call" | custom-call | tf_op jit(solution)/shard_map/pallas_call | solution.py:430

commit v5 on v4

--- a/solution.py
+++ b/solution.py
@@ -296,41 +296,41 @@
     hidden_max = jnp.max(jnp.max(hidden_peak[...], axis=0, keepdims=True), axis=1, keepdims=True) / own_in
     hidden_row = jnp.where(iota((1, 128), 1) == z, hidden_max, 0.0)
     current = jnp.where(iota((2, 128), 0) == 0, peaks[...], hidden_row)
-    def m_copy(turn, slot, peer):
-        return remote(message.at[turn], inbox.at[slot], m_send.at[slot], m_recv.at[slot], peer)
-
-    def to_hubs(act):
-        for slot, peer in enumerate(peers[0]):
-            pl.when((core + slot + 1) % CORES == 1)(functools.partial(act, m_copy(0, slot, peer)))
-
-    def hub_copy(place, slot, peer):
-        slot = len(peers[0]) + slot
-        return remote(message.at[1], inbox.at[slot], h_send.at[place], m_recv.at[slot], peer)
-
-    hub_copies = [hub_copy(to * (n_z - 1) + j, j, peers[1 + to][j]) for to in range(2) for j in range(n_z - 1)]
-    hub_copies.append(hub_copy(2 * (n_z - 1), n_z - 1, partner))
+    others = n_y * members - 1
+    chips = [(i, j) for i in range(n_y) for j in range(n_x)]
+
+    def gather_copy(index):
+        i, j = chips[index]
+        hub = ((y + i) % n_y, (z * n_x + (x + j) % n_x) * CORES + 1)
+        slot = others - (index * CORES + 1 - core)
+        return remote(message.at[0], inbox.at[slot], m_send.at[index], m_recv.at[0], hub)
+
+    def hub_copy(place, slot, peer, sem):
+        return remote(message.at[1], inbox.at[others + 1 + slot], h_send.at[place], m_recv.at[sem], peer)
+
+    def arrived(low, count, sem):
+        block = inbox.at[pl.ds(low, count)]
+        remote(block, block, m_send.at[0], m_recv.at[sem], partner).wait_recv()
+        return jnp.max(inbox[low:low + count], axis=0)
+
+    hub_copies = [hub_copy(to * (n_z - 1) + j, j, peers[1 + to][j], 1) for to in range(2) for j in range(n_z - 1)]
+    hub_copies.append(hub_copy(2 * (n_z - 1), n_z - 1, partner, 2))
     message[0] = current
-    to_hubs(lambda copy: copy.start())
+    for index in range(1, len(chips)):
+        gather_copy(index).start()
+
+    @pl.when(core == 0)
+    def _():
+        gather_copy(0).start()
+        message[1] = arrived(others + n_z, 1, 2)
 
     @pl.when(core == 1)
     def _():
-        total = message[0]
-        for slot, peer in enumerate(peers[0]):
-            m_copy(0, slot, peer).wait_recv()
-            total = jnp.maximum(total, inbox[slot])
-        message[1] = total
+        message[1] = jnp.maximum(message[0], arrived(0, others, 0))
         for copy in hub_copies:
             copy.start()
 
-    @pl.when(core == 0)
-    def _():
-        hub_copies[-1].wait_recv()
-        message[1] = inbox[len(peers[0]) + n_z - 1]
-
-    current = message[1]
-    for j in range(n_z - 1):
-        hub_copies[j].wait_recv()
-        current = jnp.maximum(current, inbox[len(peers[0]) + j])
+    current = jnp.maximum(message[1], arrived(others + 1, n_z - 1, 1))
 
     new_grad[...] = jnp.concatenate([hist_grad[...][1:], current[0:1, 0:n_z]], axis=0)
     new_hidden[...] = jnp.concatenate([hist_hidden[...][1:], current[1:2, 0:n_z]], axis=0)
@@ -352,7 +352,12 @@
         for late in range(2):
             first_copy(way, late).wait_send()
     lax.fori_loop(0, n_z, drain, 0)
-    to_hubs(lambda copy: copy.wait_send())
+    for index in range(1, len(chips)):
+        gather_copy(index).wait_send()
+
+    @pl.when(core == 0)
+    def _():
+        gather_copy(0).wait_send()
 
     @pl.when(core == 1)
     def _():
@@ -388,7 +393,7 @@
         units = down_weight.shape[1]
         capacity = tok * 9 // 32
         width = features * (capacity - MAIN) // MAIN
-        n_messages = n_y * members - 1 + n_z
+        n_messages = n_y * members + n_z
         dma = pltpu.SemaphoreType.DMA
         anywhere = pl.BlockSpec(memory_space=pl.ANY)
         vmem, hbm = pl.BlockSpec(memory_space=pltpu.VMEM), pl.BlockSpec(memory_space=pltpu.HBM)
@@ -421,7 +426,7 @@
                 dma((n_z, 2)), dma((n_z, 2)),
                 dma((n_z, 2)), dma((n_z, 2)),
                 dma((n_z, 5)), dma((n_z, 5)),
-                dma((n_messages,)), dma((n_messages,)), dma((2 * n_z - 1,)),
+                dma((n_y * n_x,)), dma((3,)), dma((2 * n_z - 1,)),
             ],
             compiler_params=pltpu.CompilerParams(
                 collective_id=0, has_side_effects=True, vmem_limit_bytes=46 * 1024 * 1024

time: 89 us -> 88.3 us (level)
  no operation moved by 1% of the time
where the time goes in v5:
time: 88.3 us; the launch traced here: 88.2 us
  Pallas kernels  87.6 us (99%)
    pallas_call x1, Pallas kernels, per_device(): pl.pallas_call(functools.partial(kernel, n_y, n_z, n_x, capacity), out_sh...  85.3 us
    pallas_call x1, Pallas kernels, per_device(): pl.pallas_call(write_out, out_shape=tuple((jax.ShapeDtypeStruct(a.shape,...  2.27 us

profile of v5, /device:TPU:1, one launch (start us, length us, event | category | flops | bytes accessed | tf_op | source)
XLA Modules:
  0.0 88.2 jit_solution(16141497685873100455)
XLA Ops:
  0.6 85.3 %shard_map.76 = (bf16[32,72,1024]{2,1,0:T(8,128)(2,1)S(1)}, f32[8,8]{1,0:T(8,128)S(1)}, f32[8,8]{1,0:T(8,128)S(1)}) custom-call(s32[2,128]{1,0:T(2,128)} %bitcast.4, f32[8,8]{1,0:T(8,128)} %hist_grad_hbm.1, f32[8,8]{1,0:T(8,128)} %hist_hidden_hbm.1, bf16[128,3072]{1,0:T(8,128)(2,1)} %grad_hbm.1, bf16[1024,3072]{1,0:T(8,128)(2,1)} %bitcast.3), custom_call_target="tpu_custom_call" | custom-call | tf_op jit(solution)/shard_map/pallas_call | solution.py:402
  86.0 2.3 %shard_map.77 = (bf16[32,72,1024]{2,1,0:T(8,128)(2,1)}, f32[8,8]{1,0:T(8,128)}, f32[8,8]{1,0:T(8,128)}) custom-call(bf16[32,72,1024]{2,1,0:T(8,128)(2,1)S(1)} %get-tuple-element.9.refs_0_, f32[8,8]{1,0:T(8,128)S(1)} %get-tuple-element.10.refs_1_, f32[8,8]{1,0:T(8,128)S(1)} %get-tuple-element.11.refs_2_), custom_call_target="tpu_custom_call" | custom-call | tf_op jit(solution)/shard_map/pallas_call | solution.py:435

commit v6 on v5

--- a/solution.py
+++ b/solution.py
@@ -156,6 +156,19 @@
             part_of(k, 0, core), part_of(k, 1 + way, core), x_send.at[k, way], x_recv.at[k, way], sides[way]
         )
 
+    def z_half(late):
+        to_z = (z - offset(1) + n_z) % n_z
+        return remote(
+            queue.at[to_z, pl.ds(late * HALF, HALF), :], part_of(1, 0, core, late * HALF, HALF),
+            z_send.at[1], z_recv.at[late], at(to_z, x, core),
+        )
+
+    def x_half(way, late):
+        return remote(
+            part_of(1, 0, core, late * HALF, HALF), part_of(1, 1 + way, core, late * HALF, HALF),
+            x_send.at[1, way], x_recv.at[1, way], sides[way],
+        )
+
     def first_copy(way, late):
         low = HALF * (way ^ late)
         return remote(
@@ -233,7 +246,9 @@
     for late in range(2):
         for way in range(2):
             first_copy(way, late).start()
-    lax.fori_loop(1, n_z, z_body, 0)
+    z_half(0).start()
+    z_half(1).start()
+    lax.fori_loop(2, n_z, z_body, 0)
     d_copy(0, 0, core).start()
     weight_in.wait()
 
@@ -275,8 +290,11 @@
     for way in range(2):
         first_copy(way, 0).wait_recv()
         f_copy(0, way).start()
-    z_copy(1).wait_recv()
-    send_own(1)
+    for late in range(2):
+        z_half(late).wait_recv()
+        x_half(0, late).start()
+        x_half(1, late).start()
+    d_copy(1, 0, core).start()
     for way in range(2):
         first_copy(way, 1).wait_recv()
         d_copy(0, 1 + way, core).start()

time: 88.3 us -> 88.3 us (level)
  no operation moved by 1% of the time
where the time goes in v6:
time: 88.3 us; the launch traced here: 88.2 us
  Pallas kernels  87.6 us (99%)
    pallas_call x1, Pallas kernels, per_device(): pl.pallas_call(functools.partial(kernel, n_y, n_z, n_x, capacity), out_sh...  85.3 us
    pallas_call x1, Pallas kernels, per_device(): pl.pallas_call(write_out, out_shape=tuple((jax.ShapeDtypeStruct(a.shape,...  2.27 us

profile of v6, /device:TPU:1, one launch (start us, length us, event | category | flops | bytes accessed | tf_op | source)
XLA Modules:
  0.0 88.2 jit_solution(6297236359083368748)
XLA Ops:
  0.6 85.3 %shard_map.76 = (bf16[32,72,1024]{2,1,0:T(8,128)(2,1)S(1)}, f32[8,8]{1,0:T(8,128)S(1)}, f32[8,8]{1,0:T(8,128)S(1)}) custom-call(s32[2,128]{1,0:T(2,128)} %bitcast.4, f32[8,8]{1,0:T(8,128)} %hist_grad_hbm.1, f32[8,8]{1,0:T(8,128)} %hist_hidden_hbm.1, bf16[128,3072]{1,0:T(8,128)(2,1)} %grad_hbm.1, bf16[1024,3072]{1,0:T(8,128)(2,1)} %bitcast.3), custom_call_target="tpu_custom_call" | custom-call | tf_op jit(solution)/shard_map/pallas_call | solution.py:420
  86.0 2.3 %shard_map.77 = (bf16[32,72,1024]{2,1,0:T(8,128)(2,1)}, f32[8,8]{1,0:T(8,128)}, f32[8,8]{1,0:T(8,128)}) custom-call(bf16[32,72,1024]{2,1,0:T(8,128)(2,1)S(1)} %get-tuple-element.9.refs_0_, f32[8,8]{1,0:T(8,128)S(1)} %get-tuple-element.10.refs_1_, f32[8,8]{1,0:T(8,128)S(1)} %get-tuple-element.11.refs_2_), custom_call_target="tpu_custom_call" | custom-call | tf_op jit(solution)/shard_map/pallas_call | solution.py:453
